TPU v7x, 32 devices: a whole 2x2x4 slice. The times are simulated.
32 devices in a mesh: row: 4 (over y, x), col: 8 (over z, core).
Axes of the slice: x: 2, y: 2, z: 4, core: 2. Of those that a mesh axis runs over, the one named last changes fastest.
Arguments:
- values: bfloat16 [4096, 4096], P('row', 'col'), may hold values from 0.0001296997 to 0.12988281
- tile_mask: int32 [32, 32], P('row', 'col'), may hold values 0 or 1
- keep_mask: int32 [32, 32], P('row', 'col'), may hold values 0 or 1
- thr_index: int32 [4096], P('col'), may hold values from 0 to 9
Outputs:
- expanded: bfloat16 [4096, 4096], P('row', 'col')
All inputs are finite; a program needn't handle non-finite values. No bound on the sum of `tile_mask` or of `keep_mask` on one device may be relied on, other than what follows from the above.
Results may differ from a plain program's by a relative error of at most 0.0004.
Values may be sent and summed in bfloat16 or wider, within the bound.
A program may use at most 64 MiB of HBM per device.

v0:
```python
import functools

import jax
import jax.numpy as jnp
from jax import lax
from jax.experimental import pallas as pl
from jax.experimental.pallas import tpu as pltpu
from jax.sharding import PartitionSpec as P

TB = 128
CORES = 2
CHUNKS = 4


def snake(index, width):
    line, spot = index // width, index % width
    return line * width + spot + (line % 2) * (width - 1 - 2 * spot)


def kernel(
    row_dev, col_dev, width, chunks, order,
    v_ref, tile_ref, keep_ref, thr_ref, acc, totals_ref,
    row_panel, col_panel, sums, stats,
    line_send, line_recv, pair_send, pair_recv, ring_send, ring_recv,
    sum_send, sum_recv, stat_send, stat_recv, loaded, load_sem, token,
):
    rows, cols = v_ref.shape
    step_rows = rows // chunks
    chips = col_dev // CORES
    half = row_dev // 2
    me_row, me_col = lax.axis_index("row"), lax.axis_index("col")
    z, core = me_col // CORES, me_col % CORES
    pos = snake(me_row, width)

    def ring_device(offset):
        return snake((pos + offset + row_dev) % row_dev, width)

    barrier = pltpu.get_barrier_semaphore()
    pl.semaphore_signal(barrier, inc=1, device_id={"col": z * CORES + 1 - core})
    peers = 1 + (z > 0).astype(jnp.int32) + (z < chips - 1).astype(jnp.int32)
    for offset in ((1, -1) if row_dev > 2 else (1,) * half):
        pl.semaphore_signal(barrier, inc=1, device_id={"row": ring_device(offset)})
        peers += 1

    @pl.when(z > 0)
    def _():
        pl.semaphore_signal(barrier, inc=1, device_id={"col": me_col - CORES})

    @pl.when(z < chips - 1)
    def _():
        pl.semaphore_signal(barrier, inc=1, device_id={"col": me_col + CORES})

    def load(q):
        spot = pl.ds(q * step_rows, step_rows)
        return pltpu.make_async_copy(v_ref.at[spot], loaded.at[spot], load_sem.at[q])

    for q in range(chunks):
        load(q).start()

    stored = tile_ref[...].astype(jnp.float32)
    kept = keep_ref[...].astype(jnp.float32)
    height = min(step_rows, TB)
    for lo in range(0, rows, height):
        if lo % step_rows == 0:
            load(lo // step_rows).wait()
        for b in range(cols // TB):
            r, c = slice(lo, lo + height), slice(b * TB, (b + 1) * TB)
            scale = jnp.broadcast_to(stored[b : b + 1, lo // TB : lo // TB + 1], (height, TB))
            tile = (loaded[r, c].astype(jnp.float32) * scale).astype(jnp.bfloat16)
            row_panel[me_col, r, c] = tile
            col_panel[pl.ds(pl.multiple_of(me_row * rows + lo, height), height), c] = tile

    pl.semaphore_wait(barrier, peers)

    def row_part(block, q):
        return row_panel.at[block, pl.ds(q * step_rows, step_rows)]

    def line_copy(zi, q, to_right):
        part = row_part(zi * CORES + core, q)
        return pltpu.make_async_remote_copy(
            src_ref=part, dst_ref=part,
            send_sem=line_send.at[to_right, zi, q], recv_sem=line_recv.at[zi, q],
            device_id={"col": me_col + (CORES if to_right else -CORES)},
        )

    def pair_copy(zi, q, lane):
        part = row_part(zi * CORES + lane, q)
        return pltpu.make_async_remote_copy(
            src_ref=part, dst_ref=part,
            send_sem=pair_send.at[zi, q], recv_sem=pair_recv.at[zi, q],
            device_id={"col": z * CORES + 1 - core},
        )

    def ring_copy(owner, q, to_right):
        start = pl.multiple_of(owner * rows + q * step_rows, step_rows)
        part = col_panel.at[pl.ds(start, step_rows)]
        return pltpu.make_async_remote_copy(
            src_ref=part, dst_ref=part,
            send_sem=ring_send.at[to_right, owner, q], recv_sem=ring_recv.at[owner, q],
            device_id={"row": ring_device(1 if to_right else -1)},
        )

    def on_ring(d, q, to_right):
        if d < half:
            return True
        return d == half and (q < chunks // 2) == bool(to_right)

    def relay(zi, q, to_right, wait):
        if wait:
            line_copy(zi, q, to_right).wait_recv()
        go = (z < chips - 1) if to_right else (z > 0)

        @pl.when(go)
        def _():
            line_copy(zi, q, to_right).start()

    for q in range(chunks):
        for to_right in (1, 0):
            relay(z, q, to_right, False)
            if on_ring(1, q, to_right):
                ring_copy(me_row, q, to_right).start()
        pair_copy(z, q, core).start()

    for to_right in (1, 0):
        first, end = (0, chips - 1) if to_right else (chips - 1, 0)

        @pl.when(z != first)
        def _():
            pl.semaphore_wait(token.at[to_right], 1)

        @pl.when(z != end)
        def _():
            pl.semaphore_signal(
                token.at[to_right], inc=1,
                device_id={"col": me_col + (CORES if to_right else -CORES)},
            )

    def line_step(t, q):
        for to_right in (1, 0):
            valid = (z >= t) if to_right else (z + t < chips)
            zi = z - t if to_right else z + t
            if t < chips:
                @pl.when(valid)
                def _():
                    relay(zi, q, to_right, True)
                    pair_copy(zi, q, core).start()

    def ring_step(t, q):
        for to_right in (1, 0):
            if on_ring(t, q, to_right):
                owner = ring_device(-t if to_right else t)
                ring_copy(owner, q, to_right).wait_recv()
                if on_ring(t + 1, q, to_right):
                    ring_copy(owner, q, to_right).start()

    def stat_copy(d):
        return pltpu.make_async_remote_copy(
            src_ref=stats.at[0], dst_ref=stats.at[d],
            send_sem=stat_send.at[d], recv_sem=stat_recv.at[d],
            device_id={"col": (me_col + d) % col_dev},
        )

    def send_stats():
        total = jnp.zeros((1, cols), jnp.float32)
        for i in range(row_dev):
            block = col_panel[i * rows : (i + 1) * rows].astype(jnp.float32)
            total += jnp.sum(block, axis=0, keepdims=True)
        stats[0] = total
        for d in range(1, col_dev):
            stat_copy(d).start()

    def product_sums():
        total = jnp.zeros((1, cols), jnp.float32)
        for d in range(col_dev):
            if d:
                stat_copy(d).wait()
            block = (me_col - d + col_dev) % col_dev
            inner = pl.ds(pl.multiple_of(block * cols, cols), cols)
            rest, terms = stats[d], []
            for _ in range(3):
                term = rest.astype(jnp.bfloat16).astype(jnp.float32)
                rest = rest - term
                terms.append(jnp.broadcast_to(term, (8, cols)))
            spread = jnp.dot(
                jnp.concatenate(terms, axis=0).astype(jnp.bfloat16), col_panel[inner],
                preferred_element_type=jnp.float32,
            )
            total += spread[16:17] + spread[8:9] + spread[0:1]
        return total

    def compute(zi, q, first=False):
        spot = pl.ds(pl.multiple_of(q * step_rows, step_rows), step_rows)
        total = None
        for lane in range(CORES):
            block = zi * CORES + lane
            inner = pl.ds(pl.multiple_of(block * cols, cols), cols)
            term = jnp.dot(
                row_panel[block, spot], col_panel[inner], preferred_element_type=jnp.float32
            )
            total = term if total is None else total + term
        if first:
            acc[spot] = total
        else:
            acc[spot] += total

    def take(zi, q, first=False):
        pair_copy(zi, q, 1 - core).wait_recv()
        compute(zi, q, first)

    def sides(t):
        return ((z >= t, z - t), (z + t < chips, z + t))

    def bulk(upto):
        @pl.loop(0, chunks)
        def _(q):
            take(z, q, True)
            for t in range(1, min(upto, chips - 1) + 1):
                for valid, zi in sides(t):
                    @pl.when(valid)
                    def _():
                        take(zi, q)

    def prune(q, cut):
        parts = []
        for b in range(cols // TB):
            c = slice(b * TB, (b + 1) * TB)
            part = jnp.zeros((1, TB), jnp.float32)
            for lo in range(q * step_rows, (q + 1) * step_rows, min(step_rows, TB)):
                r = slice(lo, lo + min(step_rows, TB))
                keep = jnp.broadcast_to(kept[b : b + 1, lo // TB : lo // TB + 1], (r.stop - lo, TB))
                pruned = jnp.maximum(acc[r, c] - cut[:, c], 0.0) * keep
                acc[r, c] = pruned
                part += jnp.sum(pruned, axis=0, keepdims=True)
            parts.append(part)
        return jnp.concatenate(parts, axis=1)

    def cuts():
        return 0.125 * thr_ref[...].astype(jnp.float32) * (product_sums() / order)

    part = jnp.zeros((1, cols), jnp.float32)
    last = max(chips - 1, half)
    if half == 0:
        send_stats()
        bulk(0)
    for t in range(1, last + 1):
        if t == half:
            for q in range(chunks):
                ring_step(t, q)
            send_stats()
            for q in range(chunks):
                line_step(t, q)
            bulk(t)
        else:
            if t == last and t > half:
                cut = cuts()
            for q in range(chunks):
                line_step(t, q)
                if t < half:
                    ring_step(t, q)
                else:
                    for valid, zi in sides(t):
                        @pl.when(valid)
                        def _():
                            take(zi, q)
                    if t == last:
                        part += prune(q, cut)
    if last <= half:
        cut = cuts()
        for q in range(chunks):
            part += prune(q, cut)

    sums[0] = part

    def sum_copy(d):
        return pltpu.make_async_remote_copy(
            src_ref=sums.at[0], dst_ref=sums.at[d],
            send_sem=sum_send.at[d], recv_sem=sum_recv.at[d],
            device_id={"row": (me_row + d) % row_dev},
        )

    for d in range(1, row_dev):
        sum_copy(d).start()
    for d in range(1, row_dev):
        sum_copy(d).wait()
        part += sums[d]
    totals_ref[...] = 1.0 / jnp.maximum(part / order, 0.1)

    for q in range(chunks):
        for zi in range(chips):
            pair_copy(zi, q, core).wait_send()

            @pl.when((z < chips - 1) & (z >= zi))
            def _():
                line_copy(zi, q, 1).wait_send()

            @pl.when((z > 0) & (z <= zi))
            def _():
                line_copy(zi, q, 0).wait_send()
        for d in range(0, half):
            for to_right in (1, 0):
                if on_ring(d + 1, q, to_right):
                    owner = ring_device(-d if to_right else d)
                    ring_copy(owner, q, to_right).wait_send()


def on_device(values, tile_mask, keep_mask, thr_index, *, row_dev, col_dev):
    rows, cols = values.shape
    width = max(w for w in range(1, row_dev + 1) if row_dev % w == 0 and w * w <= row_dev)
    chips = col_dev // CORES
    dma = pltpu.SemaphoreType.DMA
    vmem = pl.BlockSpec(memory_space=pltpu.VMEM)
    pruned, scale = pl.pallas_call(
        functools.partial(kernel, row_dev, col_dev, width, CHUNKS, rows * row_dev),
        out_shape=(
            pltpu.VMEM((rows, cols), jnp.float32),
            jax.ShapeDtypeStruct((1, cols), jnp.float32),
        ),
        in_specs=[pl.BlockSpec(memory_space=pl.ANY)] + [vmem] * 3,
        out_specs=(vmem, vmem),
        scratch_shapes=[
            pltpu.VMEM((col_dev, rows, cols), jnp.bfloat16),
            pltpu.VMEM((row_dev * rows, cols), jnp.bfloat16),
            pltpu.VMEM((row_dev, 1, cols), jnp.float32),
            pltpu.VMEM((col_dev, 1, cols), jnp.float32),
            dma((2, chips, CHUNKS)),
            dma((chips, CHUNKS)),
            dma((chips, CHUNKS)),
            dma((chips, CHUNKS)),
            dma((2, row_dev, CHUNKS)),
            dma((row_dev, CHUNKS)),
            dma((row_dev,)),
            dma((row_dev,)),
            dma((col_dev,)),
            dma((col_dev,)),
            pltpu.VMEM((rows, cols), jnp.bfloat16),
            dma((CHUNKS,)),
            pltpu.SemaphoreType.REGULAR((2,)),
        ],
        compiler_params=pltpu.CompilerParams(
            collective_id=0, has_side_effects=True,
            vmem_limit_bytes=63 * 2**20 - 4 * rows * cols + 2**19,
        ),
    )(values, tile_mask.T, keep_mask.T, thr_index.reshape(1, cols))
    return (pruned * scale).astype(jnp.bfloat16)


def solution(mesh):
    return jax.shard_map(
        functools.partial(on_device, row_dev=mesh.shape["row"], col_dev=mesh.shape["col"]),
        mesh=mesh,
        in_specs=(P("row", "col"), P("row", "col"), P("row", "col"), P("col")),
        out_specs=P("row", "col"),
        check_vma=False,
    )
```

profile of v0, /device:TPU:0, one launch (start us, length us, event | category | flops | bytes accessed | tf_op | source)
XLA Modules:
  0.0 82.7 jit_solution(12907755413188716893)
XLA Ops:
  0.0 80.8 %shard_map.46 = (f32[1024,512]{1,0:T(8,128)S(1)}, f32[1,512]{1,0:T(1,128)}) custom-call(bf16[1024,512]{1,0:T(8,128)(2,1)} %v_ref.1, s32[4,8]{1,0:T(4,128)} %bitcast.4, s32[4,8]{1,0:T(4,128)} %bitcast.5, s32[1,512]{1,0:T(1,128)} %bitcast.6), custom_call_target="tpu_custom_call" | custom-call | tf_op jit(solution)/shard_map/pallas_call | solution.py:312
  80.8 1.9 %multiply_convert_fusion = bf16[1024,512]{1,0:T(8,128)(2,1)} fusion(f32[1024,512]{1,0:T(8,128)S(1)} %get-tuple-element.7, f32[512]{0:T(512)} %bitcast.7), kind=kLoop, calls=%fused_computation | loop fusion | flops 1048576 | bytes 3147776 | tf_op jit(solution)/shard_map/convert_element_type | solution.py:344
where the time goes:
time: 82.9 us; the launch traced here: 82.7 us
  Pallas kernels  80.8 us (97%)
  other arithmetic  1.92 us (2%)
    pallas_call x1, Pallas kernels, on_device(): pl.pallas_call(functools.partial(kernel, row_dev, col_dev, width, CHUNKS,...  80.8 us
    convert_element_type x1, other arithmetic, on_device(): return (pruned * scale).astype(jnp.bfloat16)  1.92 us

commit v1 on v0

--- a/solution.py
+++ b/solution.py
@@ -303,10 +303,568 @@
                     ring_copy(owner, q, to_right).wait_send()
 
 
+def cut_rows(lo, hi):
+    while lo < hi:
+        stop = min(hi, (lo // TB + 1) * TB)
+        yield lo, stop
+        lo = stop
+
+
+def near_kernel(
+    width, bounds, order,
+    v_ref, tile_ref, keep_ref, thr_ref, acc, scale_ref,
+    row_panel, col_panel, far, done, done_in, ahead,
+    row_sums, stats, sums, far_sums, ahead_sums, notes, loaded,
+    line_send, line_recv, pair_send, pair_recv, ring_send, ring_recv,
+    far_send, far_recv, far_line_send, far_line_recv,
+    row_send, row_recv, stat_send, stat_recv, sum_send, sum_recv,
+    far_sum_send, far_sum_recv, ahead_send, ahead_recv,
+    note_send, note_recv, done_send, done_recv, load_sem,
+):
+    rows, cols = v_ref.shape
+    row_dev, col_dev, chips = row_sums.shape[0], stats.shape[0], stats.shape[0] // CORES
+    chunks = len(bounds) - 1
+    me_row, me_col = lax.axis_index("row"), lax.axis_index("col")
+    z, core = me_col // CORES, me_col % CORES
+    pos = snake(me_row, width)
+    on_right = z >= chips // 2
+    end = jnp.where(on_right, chips - 1, 0)
+    out = jnp.where(on_right, 1, -1)
+    near, over, other = end - out, end - 2 * out, end - 3 * out
+    is_end = z == end
+    is_near = z == near
+
+    def ring_device(offset):
+        return snake((pos + offset + row_dev) % row_dev, width)
+
+    opposite = ring_device(2)
+
+    barrier = pltpu.get_barrier_semaphore()
+    for d in range(1, row_dev):
+        pl.semaphore_signal(barrier, inc=1, device_id={"row": (me_row + d) % row_dev})
+    for d in range(1, col_dev):
+        pl.semaphore_signal(barrier, inc=1, device_id={"col": (me_col + d) % col_dev})
+
+    def span(q):
+        return pl.ds(bounds[q], bounds[q + 1] - bounds[q])
+
+    def block_rows(owner, q):
+        return pl.ds(pl.multiple_of(owner * rows + bounds[q], 16), bounds[q + 1] - bounds[q])
+
+    def load(q):
+        return pltpu.make_async_copy(v_ref.at[span(q)], loaded.at[span(q)], load_sem.at[q])
+
+    for q in range(chunks):
+        load(q).start()
+
+    stored = tile_ref[...].astype(jnp.float32)
+    kept = keep_ref[...].astype(jnp.float32)
+    tile_sums = [jnp.zeros((1, TB), jnp.float32) for _ in range(cols // TB)]
+    for q in range(chunks):
+        load(q).wait()
+        for lo, hi in cut_rows(bounds[q], bounds[q + 1]):
+            for b in range(cols // TB):
+                r, c = slice(lo, hi), slice(b * TB, (b + 1) * TB)
+                scale = jnp.broadcast_to(stored[b : b + 1, lo // TB : lo // TB + 1], (hi - lo, TB))
+                tile = loaded[r, c].astype(jnp.float32) * scale
+                tile_sums[b] += jnp.sum(tile, axis=0, keepdims=True)
+                tile = tile.astype(jnp.bfloat16)
+                row_panel[me_col, r, c] = tile
+                col_panel[pl.ds(pl.multiple_of(me_row * rows + lo, 16), hi - lo), c] = tile
+    row_sums[0] = jnp.concatenate(tile_sums, axis=1)
+
+    pl.semaphore_wait(barrier, row_dev + col_dev - 2)
+
+    def line(zi, q, outward):
+        part = row_panel.at[zi * CORES + core, span(q)]
+        return pltpu.make_async_remote_copy(
+            src_ref=part, dst_ref=part,
+            send_sem=line_send.at[outward, zi, q], recv_sem=line_recv.at[zi, q],
+            device_id={"col": me_col + (CORES if outward else -CORES) * out},
+        )
+
+    def pair(zi, q, lane):
+        part = row_panel.at[zi * CORES + lane, span(q)]
+        return pltpu.make_async_remote_copy(
+            src_ref=part, dst_ref=part,
+            send_sem=pair_send.at[zi, q], recv_sem=pair_recv.at[zi, q],
+            device_id={"col": z * CORES + 1 - core},
+        )
+
+    def ring(owner, q, to_right):
+        part = col_panel.at[block_rows(owner, q)]
+        return pltpu.make_async_remote_copy(
+            src_ref=part, dst_ref=part,
+            send_sem=ring_send.at[to_right, owner, q], recv_sem=ring_recv.at[owner, q],
+            device_id={"row": ring_device(1 if to_right else -1)},
+        )
+
+    def far_ring(q, to_right):
+        return pltpu.make_async_remote_copy(
+            src_ref=row_panel.at[end * CORES + core, span(q)],
+            dst_ref=far.at[block_rows(me_row, q)],
+            send_sem=far_send.at[to_right, q], recv_sem=far_recv.at[to_right, q],
+            device_id={"row": ring_device(1 if to_right else -1)},
+        )
+
+    def far_line(q):
+        part = block_rows(opposite, q)
+        return pltpu.make_async_remote_copy(
+            src_ref=col_panel.at[part], dst_ref=far.at[part],
+            send_sem=far_line_send.at[q], recv_sem=far_line_recv.at[q],
+            device_id={"col": me_col - CORES * out},
+        )
+
+    def row_sum_copy(d):
+        return pltpu.make_async_remote_copy(
+            src_ref=row_sums.at[0], dst_ref=row_sums.at[d],
+            send_sem=row_send.at[d], recv_sem=row_recv.at[d],
+            device_id={"row": (me_row + d) % row_dev},
+        )
+
+    def stat_copy(d):
+        return pltpu.make_async_remote_copy(
+            src_ref=stats.at[0], dst_ref=stats.at[d],
+            send_sem=stat_send.at[d], recv_sem=stat_recv.at[d],
+            device_id={"col": (me_col + d) % col_dev},
+        )
+
+    def sum_copy(d):
+        return pltpu.make_async_remote_copy(
+            src_ref=sums.at[0], dst_ref=sums.at[d],
+            send_sem=sum_send.at[d], recv_sem=sum_recv.at[d],
+            device_id={"row": (me_row + d) % row_dev},
+        )
+
+    def far_sum_copy(d):
+        return pltpu.make_async_remote_copy(
+            src_ref=sums.at[0], dst_ref=far_sums.at[d],
+            send_sem=far_sum_send.at[d], recv_sem=far_sum_recv.at[d],
+            device_id={"row": (me_row + d) % row_dev, "col": me_col - CORES * out},
+        )
+
+    def ahead_copy():
+        return pltpu.make_async_remote_copy(
+            src_ref=ahead_sums.at[0], dst_ref=ahead_sums.at[1],
+            send_sem=ahead_send.at[0], recv_sem=ahead_recv.at[0],
+            device_id={"col": me_col + CORES * out},
+        )
+
+    def note_copy():
+        return pltpu.make_async_remote_copy(
+            src_ref=notes.at[0], dst_ref=notes.at[1],
+            send_sem=note_send.at[0], recv_sem=note_recv.at[0],
+            device_id={"col": me_col - CORES * out},
+        )
+
+    halves = (0, done.shape[0] // 32 * 16, done.shape[0])
+
+    def done_copy(h):
+        part = pl.ds(halves[h], halves[h + 1] - halves[h])
+        return pltpu.make_async_remote_copy(
+            src_ref=done.at[part], dst_ref=done_in.at[part],
+            send_sem=done_send.at[h], recv_sem=done_recv.at[h],
+            device_id={"col": me_col + CORES * out},
+        )
+
+    def relays(q, to_right):
+        return (q % 2 == 0) == bool(to_right)
+
+    def own_ring(q):
+        for to_right in (1, 0):
+            ring(me_row, q, to_right).start()
+
+    def ring_wait(q):
+        for to_right in (1, 0):
+            ring(ring_device(-1 if to_right else 1), q, to_right).wait_recv()
+
+    def ring_relay(q):
+        for to_right in (1, 0):
+            if relays(q, to_right):
+                ring(ring_device(-1 if to_right else 1), q, to_right).start()
+
+    def ring_last(q):
+        ring(opposite, q, 1 if relays(q, 1) else 0).wait_recv()
+
+    ahead_of = chunks - 1
+    base = bounds[ahead_of]
+    raw = range(ahead_of)
+
+    for d in range(1, row_dev):
+        row_sum_copy(d).start()
+
+    @pl.when(is_end)
+    def _():
+        for q in range(chunks):
+            line(end, q, 0).start()
+            if q < 2:
+                own_ring(q)
+            if q in raw:
+                pair(end, q, core).start()
+
+    @pl.when(is_near)
+    def _():
+        for q in range(chunks):
+            if q < 2:
+                line(near, q, 0).start()
+                own_ring(q)
+            if q in raw:
+                line(near, q, 1).start()
+            pair(near, q, core).start()
+
+    def send_stats():
+        for d in range(1, row_dev):
+            row_sum_copy(d).wait()
+        total = row_sums[0]
+        for d in range(1, row_dev):
+            total += row_sums[d]
+        stats[0] = total
+        for d in range(1, col_dev):
+            stat_copy(d).start()
+
+    def wait_stats():
+        for d in range(1, col_dev):
+            stat_copy(d).wait()
+
+    def inner(owner, lane):
+        return pl.ds(pl.multiple_of((owner * CORES + lane) * cols, cols), cols)
+
+    def product_sums(owners, lanes=range(CORES)):
+        total = jnp.zeros((1, cols), jnp.float32)
+        for owner in owners:
+            for lane in lanes:
+                rest = stats[(me_col - owner * CORES - lane + col_dev) % col_dev]
+                terms = []
+                for _ in range(3):
+                    term = rest.astype(jnp.bfloat16).astype(jnp.float32)
+                    rest = rest - term
+                    terms.append(jnp.broadcast_to(term, (8, cols)))
+                spread = jnp.dot(
+                    jnp.concatenate(terms, axis=0).astype(jnp.bfloat16),
+                    col_panel[inner(owner, lane)], preferred_element_type=jnp.float32,
+                )
+                total += spread[16:17] + spread[8:9] + spread[0:1]
+        return total
+
+    def cuts(total):
+        return 0.125 * thr_ref[...].astype(jnp.float32) * (total / order)
+
+    def product(zis, q, lanes=range(CORES)):
+        total = None
+        for zi in zis:
+            for lane in lanes:
+                term = jnp.dot(
+                    row_panel[zi * CORES + lane, span(q)], col_panel[inner(zi, lane)],
+                    preferred_element_type=jnp.float32,
+                )
+                total = term if total is None else total + term
+        return total
+
+    def prune(q, cut):
+        parts = []
+        for b in range(cols // TB):
+            c = slice(b * TB, (b + 1) * TB)
+            part = jnp.zeros((1, TB), jnp.float32)
+            for lo, hi in cut_rows(bounds[q], bounds[q + 1]):
+                keep = jnp.broadcast_to(kept[b : b + 1, lo // TB : lo // TB + 1], (hi - lo, TB))
+                pruned = jnp.maximum(acc[lo:hi, c] - cut[:, c], 0.0) * keep
+                acc[lo:hi, c] = pruned
+                part += jnp.sum(pruned, axis=0, keepdims=True)
+            parts.append(part)
+        return jnp.concatenate(parts, axis=1)
+
+    def normal(total):
+        return 1.0 / jnp.maximum(total / order, 0.1)
+
+    def arrive(zi, q, relay):
+        line(zi, q, 1).wait_recv()
+        if relay is not None:
+            line(zi, q, relay).start()
+        pair(zi, q, core).start()
+
+    def met(zi, q):
+        pair(zi, q, 1 - core).wait_recv()
+
+    @pl.when(is_end)
+    def _():
+        ring_wait(0)
+        ring_relay(0)
+        own_ring(2)
+        send_stats()
+        ring_wait(1)
+        ring_relay(1)
+        own_ring(3)
+        arrive(near, 0, None)
+        arrive(near, 1, None)
+        ring_last(0)
+        far_line(0).start()
+        ring_wait(2)
+        ring_relay(2)
+        arrive(near, 2, None)
+        ring_last(1)
+        far_line(1).start()
+        ring_wait(3)
+        ring_relay(3)
+        arrive(over, 0, None)
+        arrive(over, 1, None)
+        ring_last(2)
+        far_line(2).start()
+        ring_last(3)
+        far_line(3).start()
+        arrive(other, 0, None)
+        wait_stats()
+        cut = cuts(product_sums(range(chips)))
+        note = [cut]
+        for t in range(base // TB, base // TB + 7):
+            t = min(t, rows // TB - 1)
+            line_of = [
+                jnp.broadcast_to(kept[b : b + 1, t : t + 1], (1, TB)) for b in range(cols // TB)
+            ]
+            note.append(jnp.concatenate(line_of, axis=1))
+        notes[0] = jnp.concatenate(note, axis=0)
+        for q in raw:
+            met(end, q)
+            met(near, q)
+        acc[span(2)] = product((end, near), 2)
+        note_copy().start()
+        met(over, 0)
+        met(over, 1)
+        acc[span(1)] = product((end, near, over), 1)
+        met(other, 0)
+        acc[span(0)] = product((end, near, over, other), 0)
+        part = prune(0, cut)
+        arrive(over, 2, None)
+        arrive(other, 1, None)
+        met(over, 2)
+        acc[span(2)] += product((over,), 2)
+        met(other, 1)
+        acc[span(1)] += product((other,), 1)
+        part += prune(1, cut)
+        arrive(other, 2, None)
+        met(other, 2)
+        acc[span(2)] += product((other,), 2)
+        part += prune(2, cut)
+        ahead_copy().wait_recv()
+        sums[0] = part + ahead_sums[1]
+        for d in range(row_dev):
+            far_sum_copy(d).start()
+            if d:
+                sum_copy(d).start()
+        part = sums[0]
+        for d in range(1, row_dev):
+            sum_copy(d).wait()
+            part += sums[d]
+        scale_ref[0:1] = jnp.ones((1, cols), jnp.float32)
+        scale_ref[1:2] = normal(part)
+        for h in range(2):
+            done_copy(h).wait_recv()
+            part = slice(halves[h], halves[h + 1])
+            acc[base + halves[h] : base + halves[h + 1]] = done_in[part].astype(jnp.float32)
+        note_copy().wait_send()
+        for d in range(row_dev):
+            far_sum_copy(d).wait_send()
+        for q in range(chunks):
+            line(end, q, 0).wait_send()
+            far_line(q).wait_send()
+            if q in raw:
+                for zi in range(chips):
+                    pair(zi, q, core).wait_send()
+
+    @pl.when(is_near)
+    def _():
+        def from_end(q):
+            arrive(end, q, 0)
+            if q % 2 == 0:
+                line(near, 2 + q // 2, 0).start()
+            for to_right in (1, 0):
+                far_ring(q, to_right).start()
+            if q < 2:
+                own_ring(q + 2)
+
+        def from_over(zi, q):
+            arrive(zi, q, 1 if q in raw else None)
+
+        beside = (me_row, ring_device(1), ring_device(-1))
+        from_end(0)
+        send_stats()
+        from_over(over, 0)
+        from_end(1)
+        from_over(over, 1)
+        from_end(2)
+        from_over(other, 0)
+        from_end(3)
+        ring_wait(0)
+        ring_relay(0)
+        ring_wait(1)
+        ring_relay(1)
+        from_over(over, 2)
+        ring_wait(2)
+        ring_relay(2)
+        from_over(other, 1)
+        ring_wait(3)
+        ring_relay(3)
+        from_over(other, 2)
+        for q in raw:
+            for zi in beside:
+                met(zi, q)
+            acc[span(q)] = product(beside, q)
+        from_over(over, 3)
+        from_over(other, 3)
+        for zi in (*beside, opposite):
+            met(zi, ahead_of)
+        for q in range(chunks):
+            for to_right in (1, 0):
+                far_ring(q, to_right).wait_recv()
+        total = None
+        for lane in range(CORES):
+            for owner in beside:
+                source = (
+                    row_panel[end * CORES + core, lane * cols : (lane + 1) * cols]
+                    if owner is me_row else far[inner(owner, lane)]
+                )
+                term = jnp.dot(
+                    row_panel[owner * CORES + lane, span(ahead_of)], source,
+                    preferred_element_type=jnp.float32,
+                )
+                total = term if total is None else total + term
+        ahead[...] = total
+        for q in range(chunks):
+            far_line(q).wait_recv()
+        total = ahead[...]
+        for lane in range(CORES):
+            total += jnp.dot(
+                row_panel[opposite * CORES + lane, span(ahead_of)], far[inner(opposite, lane)],
+                preferred_element_type=jnp.float32,
+            )
+        ahead[...] = total
+        note_copy().wait_recv()
+        parts = jnp.zeros((1, cols), jnp.float32)
+        for lo, hi in cut_rows(base, rows):
+            tile = lo // TB - base // TB + 1
+            pruned = jnp.maximum(ahead[lo - base : hi - base] - notes[1, 0:1], 0.0)
+            pruned *= notes[1, tile : tile + 1]
+            ahead[lo - base : hi - base] = pruned
+            parts += jnp.sum(pruned, axis=0, keepdims=True)
+        ahead_sums[0] = parts
+        ahead_copy().start()
+        acc[span(ahead_of)] = product(beside, ahead_of)
+        wait_stats()
+        head = product_sums(beside)
+        part = jnp.zeros((1, cols), jnp.float32)
+        for d in range(row_dev):
+            far_sum_copy(d).wait_recv()
+            part += far_sums[d]
+        scale = normal(part)
+        for h in range(2):
+            done[halves[h] : halves[h + 1]] = (
+                ahead[halves[h] : halves[h + 1]] * scale
+            ).astype(jnp.bfloat16)
+        for h in range(2):
+            done_copy(h).start()
+        for q in raw:
+            met(opposite, q)
+        ring_last(0)
+        ring_last(1)
+        for q in range(chunks):
+            acc[span(q)] += product((opposite,), q, (0,))
+        head += product_sums((opposite,), (0,))
+        ring_last(2)
+        ring_last(3)
+        cut = cuts(head + product_sums((opposite,), (1,)))
+        part = jnp.zeros((1, cols), jnp.float32)
+        for q in range(chunks):
+            acc[span(q)] += product((opposite,), q, (1,))
+            part += prune(q, cut)
+        sums[0] = part
+        for d in range(1, row_dev):
+            sum_copy(d).start()
+        for d in range(1, row_dev):
+            sum_copy(d).wait()
+            part += sums[d]
+        scale_ref[...] = jnp.broadcast_to(normal(part), scale_ref.shape)
+        ahead_copy().wait_send()
+        for h in range(2):
+            done_copy(h).wait_send()
+        for q in range(chunks):
+            line(near, q, 0).wait_send()
+            line(end, q, 0).wait_send()
+            if q in raw:
+                for zi in (near, over, other):
+                    line(zi, q, 1).wait_send()
+            for zi in range(chips):
+                pair(zi, q, core).wait_send()
+            for to_right in (1, 0):
+                far_ring(q, to_right).wait_send()
+
+    for q in range(chunks):
+        for to_right in (1, 0):
+            ring(me_row, q, to_right).wait_send()
+            if relays(q, to_right):
+                ring(ring_device(-1 if to_right else 1), q, to_right).wait_send()
+
+
+def near_call(values, tile_mask, keep_mask, thr_index, *, row_dev, col_dev, width):
+    rows, cols = values.shape
+    chips = col_dev // CORES
+    base = rows * 11 // 16 // 16 * 16
+    bounds = (0, cols // 32 * 16, cols, base, rows)
+    ahead = rows - base
+    chunks = len(bounds) - 1
+    dma = pltpu.SemaphoreType.DMA
+    vmem = pl.BlockSpec(memory_space=pltpu.VMEM)
+    pruned, scale = pl.pallas_call(
+        functools.partial(near_kernel, width, bounds, rows * row_dev),
+        out_shape=(
+            pltpu.VMEM((rows, cols), jnp.float32),
+            pltpu.VMEM((2, cols), jnp.float32),
+        ),
+        in_specs=[pl.BlockSpec(memory_space=pl.ANY)] + [vmem] * 3,
+        out_specs=(vmem, vmem),
+        scratch_shapes=[
+            pltpu.VMEM((col_dev, rows, cols), jnp.bfloat16),
+            pltpu.VMEM((row_dev * rows, cols), jnp.bfloat16),
+            pltpu.VMEM((row_dev * rows, cols), jnp.bfloat16),
+            pltpu.VMEM((ahead, cols), jnp.bfloat16),
+            pltpu.VMEM((ahead, cols), jnp.bfloat16),
+            pltpu.VMEM((ahead, cols), jnp.float32),
+            pltpu.VMEM((row_dev, 1, cols), jnp.float32),
+            pltpu.VMEM((col_dev, 1, cols), jnp.float32),
+            pltpu.VMEM((row_dev, 1, cols), jnp.float32),
+            pltpu.VMEM((row_dev, 1, cols), jnp.float32),
+            pltpu.VMEM((2, 1, cols), jnp.float32),
+            pltpu.VMEM((2, 8, cols), jnp.float32),
+            pltpu.VMEM((rows, cols), jnp.bfloat16),
+            dma((2, chips, chunks)), dma((chips, chunks)),
+            dma((chips, chunks)), dma((chips, chunks)),
+            dma((2, row_dev, chunks)), dma((row_dev, chunks)),
+            dma((2, chunks)), dma((2, chunks)),
+            dma((chunks,)), dma((chunks,)),
+            dma((row_dev,)), dma((row_dev,)),
+            dma((col_dev,)), dma((col_dev,)),
+            dma((row_dev,)), dma((row_dev,)),
+            dma((row_dev,)), dma((row_dev,)),
+            dma((1,)), dma((1,)),
+            dma((1,)), dma((1,)),
+            dma((2,)), dma((2,)),
+            dma((chunks,)),
+        ],
+        compiler_params=pltpu.CompilerParams(
+            collective_id=0, has_side_effects=True,
+            vmem_limit_bytes=63 * 2**20 - 4 * rows * cols + 2**19,
+        ),
+    )(values, tile_mask.T, keep_mask.T, thr_index.reshape(1, cols))
+    early = lax.broadcasted_iota(jnp.int32, (rows, 1), 0) >= base
+    return (pruned * jnp.where(early, scale[0:1], scale[1:2])).astype(jnp.bfloat16)
+
+
 def on_device(values, tile_mask, keep_mask, thr_index, *, row_dev, col_dev):
     rows, cols = values.shape
     width = max(w for w in range(1, row_dev + 1) if row_dev % w == 0 and w * w <= row_dev)
     chips = col_dev // CORES
+    if chips == 4 and row_dev == 4 and rows == CORES * cols:
+        return near_call(
+            values, tile_mask, keep_mask, thr_index, row_dev=row_dev, col_dev=col_dev, width=width
+        )
     dma = pltpu.SemaphoreType.DMA
     vmem = pl.BlockSpec(memory_space=pltpu.VMEM)
     pruned, scale = pl.pallas_call(

time: 82.9 us -> 73.2 us (0.88)
  Pallas kernels: 80.8 us -> 71.8 us
    pallas_call x1, Pallas kernels: 80.8 us -> 71.8 us  [near_call(): pl.pallas_call(functools.partial(near_kernel, width, bounds, rows * row_d...]
where the time goes in v1:
time: 73.2 us; the launch traced here: 73.1 us
  Pallas kernels  71.8 us (98%)
  other arithmetic  1.24 us (2%)
    pallas_call x1, Pallas kernels, near_call(): pl.pallas_call(functools.partial(near_kernel, width, bounds, rows * row_d...  71.8 us

profile of v1, /device:TPU:0, one launch (start us, length us, event | category | flops | bytes accessed | tf_op | source)
XLA Modules:
  0.0 73.1 jit_solution(5110171352127501901)
XLA Ops:
  0.0 71.8 %shard_map.46 = (f32[1024,512]{1,0:T(8,128)S(1)}, f32[2,512]{1,0:T(2,128)S(1)}) custom-call(bf16[1024,512]{1,0:T(8,128)(2,1)} %v_ref.1, s32[4,8]{1,0:T(4,128)} %bitcast.7, s32[4,8]{1,0:T(4,128)} %bitcast.8, s32[1,512]{1,0:T(1,128)} %bitcast.9), custom_call_target="tpu_custom_call" | custom-call | tf_op jit(solution)/shard_map/pallas_call | solution.py:815
  71.8 1.2 %multiply_convert_fusion = bf16[1024,512]{1,0:T(8,128)(2,1)} fusion(f32[1024,512]{1,0:T(8,128)S(1)} %get-tuple-element.7, f32[512]{0:T(512)S(1)} %bitcast.6, f32[512]{0:T(512)S(1)} %bitcast.5, pred[1024]{0:T(1024)(128)(4,1)S(1)} %iota_compare_fusion), kind=kLoop, calls=%fused_computation | loop fusion | flops 1572864 | bytes 3150848 | tf_op jit(solution)/shard_map/convert_element_type | solution.py:857
  (2 shorter events, 0.0 us)

commit v2 on v0

--- a/solution.py
+++ b/solution.py
@@ -303,10 +303,517 @@
                     ring_copy(owner, q, to_right).wait_send()
 
 
+def cut_rows(lo, hi):
+    while lo < hi:
+        stop = min(hi, (lo // TB + 1) * TB)
+        yield lo, stop
+        lo = stop
+
+
+def near_kernel(
+    width, bounds, split, order,
+    v_ref, tile_ref, keep_ref, thr_ref, out_ref, acc,
+    row_panel, col_panel, far, done, ahead,
+    row_sums, stats, sums, ahead_sums, total_sums, notes, loaded,
+    sent, small, line_recv, pair_recv, ring_recv, far_recv, load_sem,
+):
+    rows, cols = v_ref.shape
+    row_dev, col_dev, chips = row_sums.shape[0], stats.shape[0], stats.shape[0] // CORES
+    chunks = len(bounds) - 1
+    ahead_of = chunks - 1
+    base = bounds[ahead_of]
+    raw = range(ahead_of)
+    me_row, me_col = lax.axis_index("row"), lax.axis_index("col")
+    z, core = me_col // CORES, me_col % CORES
+    pos = snake(me_row, width)
+    on_right = z >= chips // 2
+    end = jnp.where(on_right, chips - 1, 0)
+    out = jnp.where(on_right, 1, -1)
+    near, over, other = end - out, end - 2 * out, end - 3 * out
+    is_end = z == end
+    is_near = z == near
+    inward, outward = me_col - CORES * out, me_col + CORES * out
+
+    def ring_device(offset):
+        return snake((pos + offset + row_dev) % row_dev, width)
+
+    opposite = ring_device(2)
+
+    barrier = pltpu.get_barrier_semaphore()
+    for d in range(1, row_dev):
+        pl.semaphore_signal(barrier, inc=1, device_id={"row": (me_row + d) % row_dev})
+    for d in range(1, col_dev):
+        pl.semaphore_signal(barrier, inc=1, device_id={"col": (me_col + d) % col_dev})
+
+    def span(q):
+        return pl.ds(bounds[q], bounds[q + 1] - bounds[q])
+
+    def block_rows(owner, q):
+        return pl.ds(pl.multiple_of(owner * rows + bounds[q], 16), bounds[q + 1] - bounds[q])
+
+    def load(q):
+        return pltpu.make_async_copy(v_ref.at[span(q)], loaded.at[span(q)], load_sem.at[q])
+
+    def remote(src, dst, send, recv, device):
+        return pltpu.make_async_remote_copy(
+            src_ref=src, dst_ref=dst, send_sem=send, recv_sem=recv, device_id=device
+        )
+
+    def drain(ref, sem):
+        pltpu.make_async_copy(ref, ref, sem).wait()
+
+    def line(zi, kind, q, to_end):
+        part = row_panel.at[zi * CORES + core, span(q)]
+        return remote(
+            part, part, sent.at[to_end], line_recv.at[kind, q],
+            {"col": outward if to_end else inward},
+        )
+
+    def pair(zi, q, slot):
+        part = row_panel.at[zi * CORES + core, span(q)]
+        return remote(
+            part, part, sent.at[2], pair_recv.at[slot], {"col": z * CORES + 1 - core}
+        )
+
+    def ring(owner, q, to_right, last):
+        part = col_panel.at[block_rows(owner, q)]
+        return remote(
+            part, part, sent.at[3], ring_recv.at[last, q],
+            {"row": ring_device(1 if to_right else -1)},
+        )
+
+    def far_ring(q, to_right):
+        return remote(
+            row_panel.at[end * CORES + core, span(q)], far.at[block_rows(me_row, q)],
+            sent.at[4], far_recv.at[q // 2], {"row": ring_device(1 if to_right else -1)},
+        )
+
+    def far_own(q):
+        return pltpu.make_async_copy(
+            row_panel.at[end * CORES + core, span(q)], far.at[block_rows(me_row, q)], small.at[7]
+        )
+
+    def far_line(q):
+        part = block_rows(opposite, q)
+        return remote(
+            col_panel.at[part], far.at[part], sent.at[1], far_recv.at[2 + q // 2], {"col": inward}
+        )
+
+    def row_sum_copy(d):
+        return remote(
+            row_sums.at[0], row_sums.at[d], sent.at[5], small.at[0],
+            {"row": (me_row + d) % row_dev},
+        )
+
+    def stat_copy(d):
+        return remote(
+            stats.at[0], stats.at[d], sent.at[6], small.at[1], {"col": (me_col + d) % col_dev}
+        )
+
+    def sum_copy(d):
+        return remote(
+            sums.at[0], sums.at[d], sent.at[7], small.at[2], {"row": (me_row + d) % row_dev}
+        )
+
+    def ahead_sum_copy(d):
+        return remote(
+            total_sums.at[0], ahead_sums.at[d], sent.at[8], small.at[3],
+            {"row": (me_row + d) % row_dev, "col": outward},
+        )
+
+    def total_copy():
+        return remote(
+            total_sums.at[0], total_sums.at[1], sent.at[8], small.at[3], {"col": inward}
+        )
+
+    def note_copy():
+        return remote(notes.at[0], notes.at[1], sent.at[9], small.at[4], {"col": inward})
+
+    def early_copy():
+        return remote(
+            ahead.at[pl.ds(0, split)], acc.at[pl.ds(base, split)],
+            sent.at[9], small.at[5], {"col": outward},
+        )
+
+    def done_copy():
+        return remote(
+            done, out_ref.at[pl.ds(base + split, rows - base - split)],
+            sent.at[10], small.at[6], {"col": outward},
+        )
+
+    def own_ring(q):
+        for to_right in (1, 0):
+            ring(me_row, q, to_right, 0).start()
+
+    def ring_wait(q):
+        drain(col_panel.at[pl.ds(0, 2 * (bounds[q + 1] - bounds[q]))], ring_recv.at[0, q])
+
+    def ring_relay(q, to_right):
+        ring(ring_device(-1 if to_right else 1), q, to_right, 1).start()
+
+    def ring_last(q):
+        drain(col_panel.at[pl.ds(0, bounds[q + 1] - bounds[q])], ring_recv.at[1, q])
+
+    def pair_slot(at_end, kind, q):
+        if at_end:
+            return 0 if kind == 0 else 2 * q + kind
+        return 0 if q in raw else 1 + (kind == 2)
+
+    def first_sends(q):
+        @pl.when(is_end)
+        def _():
+            line(end, 0, q, 0).start()
+            if q < 2:
+                own_ring(q)
+            if q in raw:
+                pair(end, q, pair_slot(True, 0, q)).start()
+
+        @pl.when(is_near)
+        def _():
+            if q < 2:
+                line(near, 1, q, 0).start()
+                own_ring(q)
+            if q in raw:
+                line(near, 0, q, 1).start()
+            pair(near, q, pair_slot(False, 0, q)).start()
+
+    for q in range(chunks):
+        load(q).start()
+
+    stored = tile_ref[...].astype(jnp.float32)
+    kept = keep_ref[...].astype(jnp.float32)
+    tile_sums = [jnp.zeros((1, TB), jnp.float32) for _ in range(cols // TB)]
+
+    def mask(q):
+        load(q).wait()
+        for lo, hi in cut_rows(bounds[q], bounds[q + 1]):
+            for b in range(cols // TB):
+                r, c = slice(lo, hi), slice(b * TB, (b + 1) * TB)
+                scale = jnp.broadcast_to(stored[b : b + 1, lo // TB : lo // TB + 1], (hi - lo, TB))
+                tile = loaded[r, c].astype(jnp.float32) * scale
+                tile_sums[b] += jnp.sum(tile, axis=0, keepdims=True)
+                tile = tile.astype(jnp.bfloat16)
+                row_panel[me_col, r, c] = tile
+                col_panel[pl.ds(pl.multiple_of(me_row * rows + lo, 16), hi - lo), c] = tile
+
+    mask(0)
+    mask(1)
+    pl.semaphore_wait(barrier, row_dev + col_dev - 2)
+    first_sends(0)
+    mask(2)
+    first_sends(1)
+    mask(3)
+    row_sums[0] = jnp.concatenate(tile_sums, axis=1)
+    first_sends(2)
+    for d in range(1, row_dev):
+        row_sum_copy(d).start()
+    first_sends(3)
+
+    def send_stats():
+        drain(row_sums.at[pl.ds(1, row_dev - 1)], small.at[0])
+        total = row_sums[0]
+        for d in range(1, row_dev):
+            total += row_sums[d]
+        stats[0] = total
+        for d in range(1, col_dev):
+            stat_copy(d).start()
+
+    def wait_stats():
+        drain(stats.at[pl.ds(1, col_dev - 1)], small.at[1])
+
+    def inner(owner, lane):
+        return pl.ds(pl.multiple_of((owner * CORES + lane) * cols, cols), cols)
+
+    def product_sums(owners, lanes=range(CORES)):
+        total = jnp.zeros((1, cols), jnp.float32)
+        for owner in owners:
+            for lane in lanes:
+                rest = stats[(me_col - owner * CORES - lane + col_dev) % col_dev]
+                terms = []
+                for _ in range(3):
+                    term = rest.astype(jnp.bfloat16).astype(jnp.float32)
+                    rest = rest - term
+                    terms.append(jnp.broadcast_to(term, (8, cols)))
+                spread = jnp.dot(
+                    jnp.concatenate(terms, axis=0).astype(jnp.bfloat16),
+                    col_panel[inner(owner, lane)], preferred_element_type=jnp.float32,
+                )
+                total += spread[16:17] + spread[8:9] + spread[0:1]
+        return total
+
+    def cuts(total):
+        return 0.125 * thr_ref[...].astype(jnp.float32) * (total / order)
+
+    def product(zis, q, lanes=range(CORES), panel=col_panel):
+        total = None
+        for zi in zis:
+            for lane in lanes:
+                term = jnp.dot(
+                    row_panel[zi * CORES + lane, span(q)], panel[inner(zi, lane)],
+                    preferred_element_type=jnp.float32,
+                )
+                total = term if total is None else total + term
+        return total
+
+    def prune(q, cut):
+        parts = []
+        for b in range(cols // TB):
+            c = slice(b * TB, (b + 1) * TB)
+            part = jnp.zeros((1, TB), jnp.float32)
+            for lo, hi in cut_rows(bounds[q], bounds[q + 1]):
+                keep = jnp.broadcast_to(kept[b : b + 1, lo // TB : lo // TB + 1], (hi - lo, TB))
+                pruned = jnp.maximum(acc[lo:hi, c] - cut[:, c], 0.0) * keep
+                acc[lo:hi, c] = pruned
+                part += jnp.sum(pruned, axis=0, keepdims=True)
+            parts.append(part)
+        return jnp.concatenate(parts, axis=1)
+
+    def normal(total):
+        return 1.0 / jnp.maximum(total / order, 0.1)
+
+    def all_sums():
+        drain(sums.at[pl.ds(1, row_dev - 1)], small.at[2])
+        part = sums[0]
+        for d in range(1, row_dev):
+            part += sums[d]
+        return part
+
+    @pl.when(is_end)
+    def _():
+        def arrive(kind, q):
+            zi = (near, over, other)[kind]
+            drain(row_panel.at[0, span(q)], line_recv.at[kind, q])
+            pair(zi, q, pair_slot(True, kind, q)).start()
+
+        def met(kind, q):
+            drain(row_panel.at[0, span(q)], pair_recv.at[pair_slot(True, kind, q)])
+
+        ring_wait(0)
+        ring_relay(0, 1)
+        own_ring(2)
+        ring_wait(1)
+        ring_relay(1, 0)
+        own_ring(3)
+        send_stats()
+        arrive(0, 0)
+        arrive(0, 1)
+        ring_last(0)
+        far_line(0).start()
+        ring_wait(2)
+        ring_relay(2, 1)
+        arrive(0, 2)
+        ring_last(1)
+        far_line(1).start()
+        ring_wait(3)
+        ring_relay(3, 0)
+        arrive(1, 0)
+        arrive(1, 1)
+        ring_last(2)
+        far_line(2).start()
+        ring_last(3)
+        far_line(3).start()
+        arrive(2, 0)
+        wait_stats()
+        cut = cuts(product_sums(range(chips)))
+        note = [cut]
+        for t in range(base // TB, base // TB + 7):
+            t = min(t, rows // TB - 1)
+            line_of = [
+                jnp.broadcast_to(kept[b : b + 1, t : t + 1], (1, TB)) for b in range(cols // TB)
+            ]
+            note.append(jnp.concatenate(line_of, axis=1))
+        notes[0] = jnp.concatenate(note, axis=0)
+        drain(row_panel.at[pl.ds(0, 2), pl.ds(0, base)], pair_recv.at[0])
+        acc[span(2)] = product((end, near), 2)
+        note_copy().start()
+        met(1, 0)
+        met(1, 1)
+        acc[span(1)] = product((end, near, over), 1)
+        met(2, 0)
+        acc[span(0)] = product((end, near, over, other), 0)
+        part = prune(0, cut)
+        arrive(1, 2)
+        arrive(2, 1)
+        met(1, 2)
+        acc[span(2)] += product((over,), 2)
+        met(2, 1)
+        acc[span(1)] += product((other,), 1)
+        part += prune(1, cut)
+        arrive(2, 2)
+        met(2, 2)
+        acc[span(2)] += product((other,), 2)
+        part += prune(2, cut)
+        sums[0] = part
+        for d in range(1, row_dev):
+            sum_copy(d).start()
+        part = all_sums()
+        drain(ahead_sums, small.at[3])
+        for d in range(row_dev):
+            part += ahead_sums[d]
+        total_sums[0] = part
+        total_copy().start()
+        scale = normal(part)
+        out_ref[:base] = (acc[:base] * scale).astype(jnp.bfloat16)
+        drain(ahead.at[pl.ds(0, split)], small.at[5])
+        out_ref[base : base + split] = (acc[base : base + split] * scale).astype(jnp.bfloat16)
+        drain(done, small.at[6])
+        drain(row_panel.at[0], sent.at[0])
+        drain(col_panel.at[pl.ds(0, rows)], sent.at[1])
+        drain(row_panel.at[pl.ds(0, chips), pl.ds(0, base)], sent.at[2])
+        drain(notes.at[0], sent.at[9])
+        drain(total_sums.at[0], sent.at[8])
+
+    @pl.when(is_near)
+    def _():
+        def arrive(kind, q, relay):
+            zi = (end, over, other)[kind]
+            drain(row_panel.at[0, span(q)], line_recv.at[kind, q])
+            if relay is not None:
+                line(zi, 2 if kind == 0 else kind, q, relay).start()
+            pair(zi, q, pair_slot(False, kind, q)).start()
+
+        def from_end(q):
+            arrive(0, q, 0)
+            if q % 2 == 0:
+                line(near, 1, 2 + q // 2, 0).start()
+            for to_right in (1, 0):
+                far_ring(q, to_right).start()
+            far_own(q).start()
+            if q < 2:
+                own_ring(q + 2)
+
+        def from_over(kind, q):
+            arrive(kind, q, 1 if q in raw else None)
+
+        beside = (me_row, ring_device(1), ring_device(-1))
+        from_end(0)
+        from_over(1, 0)
+        from_end(1)
+        from_over(1, 1)
+        send_stats()
+        from_end(2)
+        from_over(2, 0)
+        from_end(3)
+        ring_wait(0)
+        ring_relay(0, 1)
+        ring_wait(1)
+        ring_relay(1, 1)
+        from_over(1, 2)
+        ring_wait(2)
+        ring_relay(2, 0)
+        from_over(2, 1)
+        ring_wait(3)
+        ring_relay(3, 0)
+        from_over(2, 2)
+        drain(row_panel.at[pl.ds(0, chips), pl.ds(0, base)], pair_recv.at[0])
+        for q in raw:
+            acc[span(q)] = product(beside, q)
+        from_over(1, 3)
+        drain(row_panel.at[pl.ds(0, 3), span(ahead_of)], pair_recv.at[1])
+        drain(far.at[pl.ds(0, rows)], small.at[7])
+        drain(far.at[pl.ds(0, 2 * bounds[2])], far_recv.at[0])
+        drain(far.at[pl.ds(0, bounds[2])], far_recv.at[2])
+        ahead[...] = product((end, near, over), ahead_of, (0,), far)
+        from_over(2, 3)
+        drain(far.at[pl.ds(0, 2 * (rows - bounds[2]))], far_recv.at[1])
+        drain(far.at[pl.ds(0, rows - bounds[2])], far_recv.at[3])
+        ahead[...] += product((end, near, over), ahead_of, (1,), far)
+        drain(row_panel.at[0, span(ahead_of)], pair_recv.at[2])
+        ahead[...] += product((other,), ahead_of, range(CORES), far)
+        drain(notes.at[1], small.at[4])
+        parts = jnp.zeros((1, cols), jnp.float32)
+        for lo, hi in cut_rows(base, rows):
+            tile = lo // TB - base // TB + 1
+            pruned = jnp.maximum(ahead[lo - base : hi - base] - notes[1, 0:1], 0.0)
+            pruned *= notes[1, tile : tile + 1]
+            ahead[lo - base : hi - base] = pruned
+            parts += jnp.sum(pruned, axis=0, keepdims=True)
+        total_sums[0] = parts
+        for d in range(row_dev):
+            ahead_sum_copy(d).start()
+        early_copy().start()
+        acc[span(ahead_of)] = product(beside, ahead_of)
+        wait_stats()
+        head = product_sums(beside)
+        drain(total_sums.at[1], small.at[3])
+        scale = normal(total_sums[1])
+        done[...] = (ahead[split:] * scale).astype(jnp.bfloat16)
+        done_copy().start()
+        ring_last(0)
+        ring_last(1)
+        for q in range(chunks):
+            acc[span(q)] += product((opposite,), q, (0,))
+        head += product_sums((opposite,), (0,))
+        ring_last(2)
+        ring_last(3)
+        cut = cuts(head + product_sums((opposite,), (1,)))
+        part = jnp.zeros((1, cols), jnp.float32)
+        for q in range(chunks):
+            acc[span(q)] += product((opposite,), q, (1,))
+            part += prune(q, cut)
+        sums[0] = part
+        for d in range(1, row_dev):
+            sum_copy(d).start()
+        out_ref[...] = (acc[...] * normal(all_sums())).astype(jnp.bfloat16)
+        drain(row_panel.at[pl.ds(0, 2)], sent.at[0])
+        drain(row_panel.at[pl.ds(0, 3), pl.ds(0, base)], sent.at[1])
+        drain(row_panel.at[pl.ds(0, chips)], sent.at[2])
+        drain(far.at[pl.ds(0, 2 * rows)], sent.at[4])
+        drain(ahead_sums, sent.at[8])
+        drain(ahead.at[pl.ds(0, split)], sent.at[9])
+        drain(done, sent.at[10])
+
+    drain(col_panel.at[pl.ds(0, 3 * rows)], sent.at[3])
+    drain(row_sums.at[pl.ds(1, row_dev - 1)], sent.at[5])
+    drain(stats.at[pl.ds(1, col_dev - 1)], sent.at[6])
+    drain(sums.at[pl.ds(1, row_dev - 1)], sent.at[7])
+
+
+def near_call(values, tile_mask, keep_mask, thr_index, *, row_dev, col_dev, width):
+    rows, cols = values.shape
+    base = rows * 11 // 16 // 16 * 16
+    split = (rows - base) * 2 // 5 // 16 * 16
+    bounds = (0, cols // 32 * 16, cols, base, rows)
+    chunks = len(bounds) - 1
+    dma = pltpu.SemaphoreType.DMA
+    vmem = pl.BlockSpec(memory_space=pltpu.VMEM)
+    return pl.pallas_call(
+        functools.partial(near_kernel, width, bounds, split, rows * row_dev),
+        out_shape=pltpu.VMEM((rows, cols), jnp.bfloat16),
+        in_specs=[pl.BlockSpec(memory_space=pl.ANY)] + [vmem] * 3,
+        out_specs=vmem,
+        scratch_shapes=[
+            pltpu.VMEM((rows, cols), jnp.float32),
+            pltpu.VMEM((col_dev, rows, cols), jnp.bfloat16),
+            pltpu.VMEM((row_dev * rows, cols), jnp.bfloat16),
+            pltpu.VMEM((row_dev * rows, cols), jnp.bfloat16),
+            pltpu.VMEM((rows - base - split, cols), jnp.bfloat16),
+            pltpu.VMEM((rows - base, cols), jnp.float32),
+            pltpu.VMEM((row_dev, 1, cols), jnp.float32),
+            pltpu.VMEM((col_dev, 1, cols), jnp.float32),
+            pltpu.VMEM((row_dev, 1, cols), jnp.float32),
+            pltpu.VMEM((row_dev, 1, cols), jnp.float32),
+            pltpu.VMEM((2, 1, cols), jnp.float32),
+            pltpu.VMEM((2, 8, cols), jnp.float32),
+            pltpu.VMEM((rows, cols), jnp.bfloat16),
+            dma((11,)), dma((8,)),
+            dma((3, chunks)), dma((7,)), dma((2, chunks)), dma((4,)), dma((chunks,)),
+        ],
+        compiler_params=pltpu.CompilerParams(
+            collective_id=0, has_side_effects=True,
+            vmem_limit_bytes=63 * 2**20 - 2 * rows * cols,
+        ),
+    )(values, tile_mask.T, keep_mask.T, thr_index.reshape(1, cols))
+
+
 def on_device(values, tile_mask, keep_mask, thr_index, *, row_dev, col_dev):
     rows, cols = values.shape
     width = max(w for w in range(1, row_dev + 1) if row_dev % w == 0 and w * w <= row_dev)
     chips = col_dev // CORES
+    if chips == 4 and row_dev == 4 and rows == CORES * cols:
+        return near_call(
+            values, tile_mask, keep_mask, thr_index, row_dev=row_dev, col_dev=col_dev, width=width
+        )
     dma = pltpu.SemaphoreType.DMA
     vmem = pl.BlockSpec(memory_space=pltpu.VMEM)
     pruned, scale = pl.pallas_call(

time: 82.9 us -> 68.8 us (0.83)
  Pallas kernels: 80.8 us -> 67.6 us
  other arithmetic: 1.92 us -> 0 us
  local copies, waits for them, and re-layouts: 0 us -> 0.97 us
    pallas_call x1, Pallas kernels: 80.8 us -> 67.6 us  [near_call(): pl.pallas_call(functools.partial(near_kernel, width, bounds, split, rows...]
    convert_element_type x1 -> x0, other arithmetic: 1.92 us -> none  [on_device(): return (pruned * scale).astype(jnp.bfloat16)]
    unnamed x0 -> x1, local copies, waits for them, and re-layouts: none -> 0.97 us
where the time goes in v2:
time: 68.8 us; the launch traced here: 68.6 us
  Pallas kernels  67.6 us (98%)
  local copies, waits for them, and re-layouts  0.97 us (1%)
    pallas_call x1, Pallas kernels, near_call(): pl.pallas_call(functools.partial(near_kernel, width, bounds, split, rows...  67.6 us

profile of v2, /device:TPU:0, one launch (start us, length us, event | category | flops | bytes accessed | tf_op | source)
XLA Modules:
  0.0 68.6 jit_solution(9990294359380066526)
XLA Ops:
  0.0 67.6 %shard_map.46 = bf16[1024,512]{1,0:T(8,128)(2,1)S(1)} custom-call(bf16[1024,512]{1,0:T(8,128)(2,1)} %v_ref.1, s32[4,8]{1,0:T(4,128)} %bitcast.3, s32[4,8]{1,0:T(4,128)} %bitcast.4, s32[1,512]{1,0:T(1,128)} %bitcast.5), custom_call_target="tpu_custom_call" | custom-call | tf_op jit(solution)/shard_map/pallas_call | solution.py:780
  67.6 1.0 %copy.6 = bf16[1024,512]{1,0:T(8,128)(2,1)} copy(bf16[1024,512]{1,0:T(8,128)(2,1)S(1)} %shard_map.46) | data formatting | bytes 2097152

commit v3 on v2

--- a/solution.py
+++ b/solution.py
@@ -312,10 +312,10 @@
 
 def near_kernel(
     width, bounds, split, order,
-    v_ref, tile_ref, keep_ref, thr_ref, out_ref, acc,
-    row_panel, col_panel, far, done, ahead,
+    v_ref, tile_hbm, keep_hbm, thr_hbm, out_ref, acc, tile_ref, keep_ref, thr_ref,
+    row_panel, col_panel, far, done, ahead, detour,
     row_sums, stats, sums, ahead_sums, total_sums, notes, loaded,
-    sent, small, line_recv, pair_recv, ring_recv, far_recv, load_sem,
+    sent, small, line_recv, pair_recv, ring_recv, far_recv, load_sem, token,
 ):
     rows, cols = v_ref.shape
     row_dev, col_dev, chips = row_sums.shape[0], stats.shape[0], stats.shape[0] // CORES
@@ -342,8 +342,13 @@
     barrier = pltpu.get_barrier_semaphore()
     for d in range(1, row_dev):
         pl.semaphore_signal(barrier, inc=1, device_id={"row": (me_row + d) % row_dev})
-    for d in range(1, col_dev):
-        pl.semaphore_signal(barrier, inc=1, device_id={"col": (me_col + d) % col_dev})
+    pl.semaphore_signal(barrier, inc=1, device_id={"col": z * CORES + 1 - core})
+    pl.semaphore_signal(barrier, inc=1, device_id={"col": inward})
+
+    @pl.when(is_near)
+    def _():
+        pl.semaphore_signal(barrier, inc=1, device_id={"col": outward})
+
 
     def span(q):
         return pl.ds(bounds[q], bounds[q + 1] - bounds[q])
@@ -399,6 +404,18 @@
             col_panel.at[part], far.at[part], sent.at[1], far_recv.at[2 + q // 2], {"col": inward}
         )
 
+    def detour_cross():
+        return remote(
+            row_panel.at[near * CORES + core, span(0)], detour, sent.at[4], small.at[8],
+            {"row": opposite},
+        )
+
+    def detour_down():
+        return remote(
+            detour, col_panel.at[block_rows(opposite, 0)], sent.at[10], ring_recv.at[1, 0],
+            {"col": inward},
+        )
+
     def row_sum_copy(d):
         return remote(
             row_sums.at[0], row_sums.at[d], sent.at[5], small.at[0],
@@ -447,6 +464,17 @@
 
     def ring_wait(q):
         drain(col_panel.at[pl.ds(0, 2 * (bounds[q + 1] - bounds[q]))], ring_recv.at[0, q])
+
+    def ring_relay_both(q):
+        middle = (bounds[q] + bounds[q + 1]) // 32 * 16
+        for to_right in (1, 0):
+            lo, hi = (bounds[q], middle) if to_right else (middle, bounds[q + 1])
+            owner = ring_device(-1 if to_right else 1)
+            part = col_panel.at[pl.ds(pl.multiple_of(owner * rows + lo, 16), hi - lo)]
+            remote(
+                part, part, sent.at[3], ring_recv.at[1, q],
+                {"row": ring_device(1 if to_right else -1)},
+            ).start()
 
     def ring_relay(q, to_right):
         ring(ring_device(-1 if to_right else 1), q, to_right, 1).start()
@@ -463,7 +491,7 @@
         @pl.when(is_end)
         def _():
             line(end, 0, q, 0).start()
-            if q < 2:
+            if q in (0, ahead_of):
                 own_ring(q)
             if q in raw:
                 pair(end, q, pair_slot(True, 0, q)).start()
@@ -477,8 +505,19 @@
                 line(near, 0, q, 1).start()
             pair(near, q, pair_slot(False, 0, q)).start()
 
-    for q in range(chunks):
+    tables = [
+        pltpu.make_async_copy(src, dst, load_sem.at[chunks + i])
+        for i, (src, dst) in enumerate(
+            ((tile_hbm, tile_ref), (keep_hbm, keep_ref), (thr_hbm, thr_ref))
+        )
+    ]
+    load(0).start()
+    for table in tables:
+        table.start()
+    for q in range(1, chunks):
         load(q).start()
+    for table in tables:
+        table.wait()
 
     stored = tile_ref[...].astype(jnp.float32)
     kept = keep_ref[...].astype(jnp.float32)
@@ -498,7 +537,12 @@
 
     mask(0)
     mask(1)
-    pl.semaphore_wait(barrier, row_dev + col_dev - 2)
+    pl.semaphore_wait(barrier, row_dev + 1 + is_near.astype(jnp.int32))
+
+    @pl.when(is_end)
+    def _():
+        pl.semaphore_signal(token.at[0], inc=1, device_id={"col": inward})
+
     first_sends(0)
     mask(2)
     first_sends(1)
@@ -590,29 +634,31 @@
 
         ring_wait(0)
         ring_relay(0, 1)
-        own_ring(2)
-        ring_wait(1)
-        ring_relay(1, 0)
-        own_ring(3)
-        send_stats()
+        own_ring(1)
         arrive(0, 0)
         arrive(0, 1)
+        ring_wait(3)
+        ring_relay(3, 0)
+        own_ring(2)
+        arrive(0, 2)
         ring_last(0)
         far_line(0).start()
+        pl.semaphore_wait(token.at[1], 1)
+        send_stats()
+        arrive(1, 0)
+        ring_wait(1)
+        ring_relay(1, 1)
+        ring_last(3)
+        far_line(3).start()
+        arrive(1, 1)
         ring_wait(2)
-        ring_relay(2, 1)
-        arrive(0, 2)
+        ring_relay(2, 0)
+        detour_cross().start()
         ring_last(1)
         far_line(1).start()
-        ring_wait(3)
-        ring_relay(3, 0)
-        arrive(1, 0)
-        arrive(1, 1)
+        arrive(2, 0)
         ring_last(2)
         far_line(2).start()
-        ring_last(3)
-        far_line(3).start()
-        arrive(2, 0)
         wait_stats()
         cut = cuts(product_sums(range(chips)))
         note = [cut]
@@ -632,6 +678,8 @@
         met(2, 0)
         acc[span(0)] = product((end, near, over, other), 0)
         part = prune(0, cut)
+        drain(detour, small.at[8])
+        detour_down().start()
         arrive(1, 2)
         arrive(2, 1)
         met(1, 2)
@@ -662,6 +710,9 @@
         drain(row_panel.at[pl.ds(0, chips), pl.ds(0, base)], sent.at[2])
         drain(notes.at[0], sent.at[9])
         drain(total_sums.at[0], sent.at[8])
+        drain(col_panel.at[pl.ds(0, 3 * rows)], sent.at[3])
+        drain(detour, sent.at[4])
+        drain(detour, sent.at[10])
 
     @pl.when(is_near)
     def _():
@@ -687,20 +738,23 @@
 
         beside = (me_row, ring_device(1), ring_device(-1))
         from_end(0)
+        pl.semaphore_wait(token.at[0], 1)
+        pl.semaphore_signal(token.at[1], inc=1, device_id={"col": inward})
         from_over(1, 0)
         from_end(1)
         from_over(1, 1)
+        pl.semaphore_wait(token.at[1], 1)
+        pl.semaphore_signal(token.at[1], inc=1, device_id={"col": outward})
         send_stats()
         from_end(2)
         from_over(2, 0)
         from_end(3)
         ring_wait(0)
-        ring_relay(0, 1)
         ring_wait(1)
         ring_relay(1, 1)
         from_over(1, 2)
         ring_wait(2)
-        ring_relay(2, 0)
+        ring_relay_both(2)
         from_over(2, 1)
         ring_wait(3)
         ring_relay(3, 0)
@@ -735,15 +789,15 @@
         acc[span(ahead_of)] = product(beside, ahead_of)
         wait_stats()
         head = product_sums(beside)
+        ring_last(1)
+        ring_last(0)
+        for q in range(chunks):
+            acc[span(q)] += product((opposite,), q, (0,))
+        head += product_sums((opposite,), (0,))
         drain(total_sums.at[1], small.at[3])
         scale = normal(total_sums[1])
         done[...] = (ahead[split:] * scale).astype(jnp.bfloat16)
         done_copy().start()
-        ring_last(0)
-        ring_last(1)
-        for q in range(chunks):
-            acc[span(q)] += product((opposite,), q, (0,))
-        head += product_sums((opposite,), (0,))
         ring_last(2)
         ring_last(3)
         cut = cuts(head + product_sums((opposite,), (1,)))
@@ -762,8 +816,8 @@
         drain(ahead_sums, sent.at[8])
         drain(ahead.at[pl.ds(0, split)], sent.at[9])
         drain(done, sent.at[10])
-
-    drain(col_panel.at[pl.ds(0, 3 * rows)], sent.at[3])
+        drain(col_panel.at[pl.ds(0, 3 * rows - bounds[1])], sent.at[3])
+
     drain(row_sums.at[pl.ds(1, row_dev - 1)], sent.at[5])
     drain(stats.at[pl.ds(1, col_dev - 1)], sent.at[6])
     drain(sums.at[pl.ds(1, row_dev - 1)], sent.at[7])
@@ -771,8 +825,8 @@
 
 def near_call(values, tile_mask, keep_mask, thr_index, *, row_dev, col_dev, width):
     rows, cols = values.shape
-    base = rows * 11 // 16 // 16 * 16
-    split = (rows - base) * 2 // 5 // 16 * 16
+    base = rows * 45 // 64 // 16 * 16
+    split = (rows - base) // 32 * 16
     bounds = (0, cols // 32 * 16, cols, base, rows)
     chunks = len(bounds) - 1
     dma = pltpu.SemaphoreType.DMA
@@ -780,15 +834,19 @@
     return pl.pallas_call(
         functools.partial(near_kernel, width, bounds, split, rows * row_dev),
         out_shape=pltpu.VMEM((rows, cols), jnp.bfloat16),
-        in_specs=[pl.BlockSpec(memory_space=pl.ANY)] + [vmem] * 3,
+        in_specs=[pl.BlockSpec(memory_space=pl.ANY)] * 4,
         out_specs=vmem,
         scratch_shapes=[
             pltpu.VMEM((rows, cols), jnp.float32),
+            pltpu.VMEM(tile_mask.shape[::-1], jnp.int32),
+            pltpu.VMEM(keep_mask.shape[::-1], jnp.int32),
+            pltpu.VMEM((1, cols), jnp.int32),
             pltpu.VMEM((col_dev, rows, cols), jnp.bfloat16),
             pltpu.VMEM((row_dev * rows, cols), jnp.bfloat16),
             pltpu.VMEM((row_dev * rows, cols), jnp.bfloat16),
             pltpu.VMEM((rows - base - split, cols), jnp.bfloat16),
             pltpu.VMEM((rows - base, cols), jnp.float32),
+            pltpu.VMEM((bounds[1], cols), jnp.bfloat16),
             pltpu.VMEM((row_dev, 1, cols), jnp.float32),
             pltpu.VMEM((col_dev, 1, cols), jnp.float32),
             pltpu.VMEM((row_dev, 1, cols), jnp.float32),
@@ -796,8 +854,9 @@
             pltpu.VMEM((2, 1, cols), jnp.float32),
             pltpu.VMEM((2, 8, cols), jnp.float32),
             pltpu.VMEM((rows, cols), jnp.bfloat16),
-            dma((11,)), dma((8,)),
-            dma((3, chunks)), dma((7,)), dma((2, chunks)), dma((4,)), dma((chunks,)),
+            dma((11,)), dma((9,)),
+            dma((3, chunks)), dma((7,)), dma((2, chunks)), dma((4,)), dma((chunks + 3,)),
+            pltpu.SemaphoreType.REGULAR((2,)),
         ],
         compiler_params=pltpu.CompilerParams(
             collective_id=0, has_side_effects=True,

time: 68.8 us -> 67.2 us (0.977)
  Pallas kernels: 67.6 us -> 66 us
    pallas_call x1, Pallas kernels: 67.6 us -> 66 us  [near_call(): pl.pallas_call(functools.partial(near_kernel, width, bounds, split, rows...]
where the time goes in v3:
time: 67.2 us; the launch traced here: 67 us
  Pallas kernels  66 us (98%)
  local copies, waits for them, and re-layouts  0.97 us (1%)
    pallas_call x1, Pallas kernels, near_call(): pl.pallas_call(functools.partial(near_kernel, width, bounds, split, rows...  66 us

profile of v3, /device:TPU:0, one launch (start us, length us, event | category | flops | bytes accessed | tf_op | source)
XLA Modules:
  0.0 67.0 jit_solution(5536337489105110324)
XLA Ops:
  0.0 66.0 %shard_map.46 = bf16[1024,512]{1,0:T(8,128)(2,1)S(1)} custom-call(bf16[1024,512]{1,0:T(8,128)(2,1)} %v_ref.1, s32[4,8]{1,0:T(4,128)} %bitcast.3, s32[4,8]{1,0:T(4,128)} %bitcast.4, s32[1,512]{1,0:T(1,128)} %bitcast.5), custom_call_target="tpu_custom_call" | custom-call | tf_op jit(solution)/shard_map/pallas_call | solution.py:834
  66.0 1.0 %copy.6 = bf16[1024,512]{1,0:T(8,128)(2,1)} copy(bf16[1024,512]{1,0:T(8,128)(2,1)S(1)} %shard_map.46) | data formatting | bytes 2097152

commit v4 on v3

--- a/solution.py
+++ b/solution.py
@@ -314,7 +314,7 @@
     width, bounds, split, order,
     v_ref, tile_hbm, keep_hbm, thr_hbm, out_ref, acc, tile_ref, keep_ref, thr_ref,
     row_panel, col_panel, far, done, ahead, detour,
-    row_sums, stats, sums, ahead_sums, total_sums, notes, loaded,
+    row_sums, stats, sums, raw_sums, ahead_sums, total_sums, notes, loaded,
     sent, small, line_recv, pair_recv, ring_recv, far_recv, load_sem, token,
 ):
     rows, cols = v_ref.shape
@@ -432,15 +432,22 @@
             sums.at[0], sums.at[d], sent.at[7], small.at[2], {"row": (me_row + d) % row_dev}
         )
 
+    def raw_sum_copy(d):
+        return remote(
+            sums.at[0], raw_sums.at[d], sent.at[11], small.at[9],
+            {"row": (me_row + d) % row_dev, "col": inward},
+        )
+
     def ahead_sum_copy(d):
         return remote(
             total_sums.at[0], ahead_sums.at[d], sent.at[8], small.at[3],
             {"row": (me_row + d) % row_dev, "col": outward},
         )
 
-    def total_copy():
-        return remote(
-            total_sums.at[0], total_sums.at[1], sent.at[8], small.at[3], {"col": inward}
+    def beside_sum_copy(d):
+        return remote(
+            total_sums.at[0], total_sums.at[d], sent.at[12], small.at[10],
+            {"row": (me_row + d) % row_dev},
         )
 
     def note_copy():
@@ -692,14 +699,14 @@
         acc[span(2)] += product((other,), 2)
         part += prune(2, cut)
         sums[0] = part
+        for d in range(row_dev):
+            raw_sum_copy(d).start()
         for d in range(1, row_dev):
             sum_copy(d).start()
+        drain(ahead_sums, small.at[3])
         part = all_sums()
-        drain(ahead_sums, small.at[3])
         for d in range(row_dev):
             part += ahead_sums[d]
-        total_sums[0] = part
-        total_copy().start()
         scale = normal(part)
         out_ref[:base] = (acc[:base] * scale).astype(jnp.bfloat16)
         drain(ahead.at[pl.ds(0, split)], small.at[5])
@@ -709,7 +716,7 @@
         drain(col_panel.at[pl.ds(0, rows)], sent.at[1])
         drain(row_panel.at[pl.ds(0, chips), pl.ds(0, base)], sent.at[2])
         drain(notes.at[0], sent.at[9])
-        drain(total_sums.at[0], sent.at[8])
+        drain(raw_sums, sent.at[11])
         drain(col_panel.at[pl.ds(0, 3 * rows)], sent.at[3])
         drain(detour, sent.at[4])
         drain(detour, sent.at[10])
@@ -754,7 +761,6 @@
         ring_relay(1, 1)
         from_over(1, 2)
         ring_wait(2)
-        ring_relay_both(2)
         from_over(2, 1)
         ring_wait(3)
         ring_relay(3, 0)
@@ -783,6 +789,9 @@
             ahead[lo - base : hi - base] = pruned
             parts += jnp.sum(pruned, axis=0, keepdims=True)
         total_sums[0] = parts
+        for d in range(1, row_dev):
+            beside_sum_copy(d).start()
+        ring_relay_both(2)
         for d in range(row_dev):
             ahead_sum_copy(d).start()
         early_copy().start()
@@ -794,8 +803,12 @@
         for q in range(chunks):
             acc[span(q)] += product((opposite,), q, (0,))
         head += product_sums((opposite,), (0,))
-        drain(total_sums.at[1], small.at[3])
-        scale = normal(total_sums[1])
+        drain(total_sums.at[pl.ds(1, row_dev - 1)], small.at[10])
+        drain(raw_sums, small.at[9])
+        part = total_sums[0] + raw_sums[0]
+        for d in range(1, row_dev):
+            part += total_sums[d] + raw_sums[d]
+        scale = normal(part)
         done[...] = (ahead[split:] * scale).astype(jnp.bfloat16)
         done_copy().start()
         ring_last(2)
@@ -814,6 +827,7 @@
         drain(row_panel.at[pl.ds(0, chips)], sent.at[2])
         drain(far.at[pl.ds(0, 2 * rows)], sent.at[4])
         drain(ahead_sums, sent.at[8])
+        drain(total_sums.at[pl.ds(1, row_dev - 1)], sent.at[12])
         drain(ahead.at[pl.ds(0, split)], sent.at[9])
         drain(done, sent.at[10])
         drain(col_panel.at[pl.ds(0, 3 * rows - bounds[1])], sent.at[3])
@@ -826,7 +840,7 @@
 def near_call(values, tile_mask, keep_mask, thr_index, *, row_dev, col_dev, width):
     rows, cols = values.shape
     base = rows * 45 // 64 // 16 * 16
-    split = (rows - base) // 32 * 16
+    split = (rows - base) * 3 // 8 // 16 * 16
     bounds = (0, cols // 32 * 16, cols, base, rows)
     chunks = len(bounds) - 1
     dma = pltpu.SemaphoreType.DMA
@@ -851,10 +865,11 @@
             pltpu.VMEM((col_dev, 1, cols), jnp.float32),
             pltpu.VMEM((row_dev, 1, cols), jnp.float32),
             pltpu.VMEM((row_dev, 1, cols), jnp.float32),
-            pltpu.VMEM((2, 1, cols), jnp.float32),
+            pltpu.VMEM((row_dev, 1, cols), jnp.float32),
+            pltpu.VMEM((row_dev, 1, cols), jnp.float32),
             pltpu.VMEM((2, 8, cols), jnp.float32),
             pltpu.VMEM((rows, cols), jnp.bfloat16),
-            dma((11,)), dma((9,)),
+            dma((13,)), dma((11,)),
             dma((3, chunks)), dma((7,)), dma((2, chunks)), dma((4,)), dma((chunks + 3,)),
             pltpu.SemaphoreType.REGULAR((2,)),
         ],

time: 67.2 us -> 66.5 us (0.990)
  no operation moved by 1% of the time
where the time goes in v4:
time: 66.5 us; the launch traced here: 66.4 us
  Pallas kernels  65.4 us (98%)
  local copies, waits for them, and re-layouts  0.97 us (1%)
    pallas_call x1, Pallas kernels, near_call(): pl.pallas_call(functools.partial(near_kernel, width, bounds, split, rows...  65.4 us

profile of v4, /device:TPU:0, one launch (start us, length us, event | category | flops | bytes accessed | tf_op | source)
XLA Modules:
  0.0 66.4 jit_solution(17383126810846788)
XLA Ops:
  0.0 65.4 %shard_map.46 = bf16[1024,512]{1,0:T(8,128)(2,1)S(1)} custom-call(bf16[1024,512]{1,0:T(8,128)(2,1)} %v_ref.1, s32[4,8]{1,0:T(4,128)} %bitcast.3, s32[4,8]{1,0:T(4,128)} %bitcast.4, s32[1,512]{1,0:T(1,128)} %bitcast.5), custom_call_target="tpu_custom_call" | custom-call | tf_op jit(solution)/shard_map/pallas_call | solution.py:848
  65.4 1.0 %copy.6 = bf16[1024,512]{1,0:T(8,128)(2,1)} copy(bf16[1024,512]{1,0:T(8,128)(2,1)S(1)} %shard_map.46) | data formatting | bytes 2097152

commit v5 on v4

--- a/solution.py
+++ b/solution.py
@@ -311,7 +311,7 @@
 
 
 def near_kernel(
-    width, bounds, split, order,
+    width, bounds, splits, order,
     v_ref, tile_hbm, keep_hbm, thr_hbm, out_ref, acc, tile_ref, keep_ref, thr_ref,
     row_panel, col_panel, far, done, ahead, detour,
     row_sums, stats, sums, raw_sums, ahead_sums, total_sums, notes, loaded,
@@ -453,17 +453,22 @@
     def note_copy():
         return remote(notes.at[0], notes.at[1], sent.at[9], small.at[4], {"col": inward})
 
-    def early_copy():
-        return remote(
-            ahead.at[pl.ds(0, split)], acc.at[pl.ds(base, split)],
+    def early_copy(c):
+        return remote(
+            ahead.at[pl.ds(0, splits[c])], acc.at[pl.ds(base, splits[c])],
             sent.at[9], small.at[5], {"col": outward},
         )
 
-    def done_copy():
-        return remote(
-            done, out_ref.at[pl.ds(base + split, rows - base - split)],
+    def done_copy(c):
+        return remote(
+            done.at[pl.ds(splits[c], rows - base - splits[c])],
+            out_ref.at[pl.ds(base + splits[c], rows - base - splits[c])],
             sent.at[10], small.at[6], {"col": outward},
         )
+
+    def on_core(act):
+        for c in range(CORES):
+            pl.when(core == c)(functools.partial(act, c))
 
     def own_ring(q):
         for to_right in (1, 0):
@@ -709,9 +714,14 @@
             part += ahead_sums[d]
         scale = normal(part)
         out_ref[:base] = (acc[:base] * scale).astype(jnp.bfloat16)
-        drain(ahead.at[pl.ds(0, split)], small.at[5])
-        out_ref[base : base + split] = (acc[base : base + split] * scale).astype(jnp.bfloat16)
-        drain(done, small.at[6])
+
+        def finish(c):
+            stop = base + splits[c]
+            drain(ahead.at[pl.ds(0, splits[c])], small.at[5])
+            out_ref[base:stop] = (acc[base:stop] * scale).astype(jnp.bfloat16)
+            drain(done.at[pl.ds(splits[c], rows - stop)], small.at[6])
+
+        on_core(finish)
         drain(row_panel.at[0], sent.at[0])
         drain(col_panel.at[pl.ds(0, rows)], sent.at[1])
         drain(row_panel.at[pl.ds(0, chips), pl.ds(0, base)], sent.at[2])
@@ -774,13 +784,14 @@
         drain(far.at[pl.ds(0, 2 * bounds[2])], far_recv.at[0])
         drain(far.at[pl.ds(0, bounds[2])], far_recv.at[2])
         ahead[...] = product((end, near, over), ahead_of, (0,), far)
-        from_over(2, 3)
+        drain(notes.at[1], small.at[4])
         drain(far.at[pl.ds(0, 2 * (rows - bounds[2]))], far_recv.at[1])
         drain(far.at[pl.ds(0, rows - bounds[2])], far_recv.at[3])
         ahead[...] += product((end, near, over), ahead_of, (1,), far)
+        from_over(2, 3)
+        ahead[...] += product((other,), ahead_of, (core,), far)
         drain(row_panel.at[0, span(ahead_of)], pair_recv.at[2])
-        ahead[...] += product((other,), ahead_of, range(CORES), far)
-        drain(notes.at[1], small.at[4])
+        ahead[...] += product((other,), ahead_of, (1 - core,), far)
         parts = jnp.zeros((1, cols), jnp.float32)
         for lo, hi in cut_rows(base, rows):
             tile = lo // TB - base // TB + 1
@@ -794,7 +805,7 @@
         ring_relay_both(2)
         for d in range(row_dev):
             ahead_sum_copy(d).start()
-        early_copy().start()
+        on_core(lambda c: early_copy(c).start())
         acc[span(ahead_of)] = product(beside, ahead_of)
         wait_stats()
         head = product_sums(beside)
@@ -809,8 +820,9 @@
         for d in range(1, row_dev):
             part += total_sums[d] + raw_sums[d]
         scale = normal(part)
-        done[...] = (ahead[split:] * scale).astype(jnp.bfloat16)
-        done_copy().start()
+        first = min(splits)
+        done[first:] = (ahead[first:] * scale).astype(jnp.bfloat16)
+        on_core(lambda c: done_copy(c).start())
         ring_last(2)
         ring_last(3)
         cut = cuts(head + product_sums((opposite,), (1,)))
@@ -828,8 +840,12 @@
         drain(far.at[pl.ds(0, 2 * rows)], sent.at[4])
         drain(ahead_sums, sent.at[8])
         drain(total_sums.at[pl.ds(1, row_dev - 1)], sent.at[12])
-        drain(ahead.at[pl.ds(0, split)], sent.at[9])
-        drain(done, sent.at[10])
+
+        def drain_ahead(c):
+            drain(ahead.at[pl.ds(0, splits[c])], sent.at[9])
+            drain(done.at[pl.ds(splits[c], rows - base - splits[c])], sent.at[10])
+
+        on_core(drain_ahead)
         drain(col_panel.at[pl.ds(0, 3 * rows - bounds[1])], sent.at[3])
 
     drain(row_sums.at[pl.ds(1, row_dev - 1)], sent.at[5])
@@ -840,13 +856,13 @@
 def near_call(values, tile_mask, keep_mask, thr_index, *, row_dev, col_dev, width):
     rows, cols = values.shape
     base = rows * 45 // 64 // 16 * 16
-    split = (rows - base) * 3 // 8 // 16 * 16
+    splits = tuple((rows - base) * n // 16 // 16 * 16 for n in (7, 3))
     bounds = (0, cols // 32 * 16, cols, base, rows)
     chunks = len(bounds) - 1
     dma = pltpu.SemaphoreType.DMA
     vmem = pl.BlockSpec(memory_space=pltpu.VMEM)
     return pl.pallas_call(
-        functools.partial(near_kernel, width, bounds, split, rows * row_dev),
+        functools.partial(near_kernel, width, bounds, splits, rows * row_dev),
         out_shape=pltpu.VMEM((rows, cols), jnp.bfloat16),
         in_specs=[pl.BlockSpec(memory_space=pl.ANY)] * 4,
         out_specs=vmem,
@@ -858,7 +874,7 @@
             pltpu.VMEM((col_dev, rows, cols), jnp.bfloat16),
             pltpu.VMEM((row_dev * rows, cols), jnp.bfloat16),
             pltpu.VMEM((row_dev * rows, cols), jnp.bfloat16),
-            pltpu.VMEM((rows - base - split, cols), jnp.bfloat16),
+            pltpu.VMEM((rows - base, cols), jnp.bfloat16),
             pltpu.VMEM((rows - base, cols), jnp.float32),
             pltpu.VMEM((bounds[1], cols), jnp.bfloat16),
             pltpu.VMEM((row_dev, 1, cols), jnp.float32),

time: 66.5 us -> 66 us (level)
  no operation moved by 1% of the time
where the time goes in v5:
time: 66 us; the launch traced here: 65.8 us
  Pallas kernels  64.8 us (98%)
  local copies, waits for them, and re-layouts  0.97 us (1%)
    pallas_call x1, Pallas kernels, near_call(): pl.pallas_call(functools.partial(near_kernel, width, bounds, splits, rows...  64.8 us

profile of v5, /device:TPU:0, one launch (start us, length us, event | category | flops | bytes accessed | tf_op | source)
XLA Modules:
  0.0 65.8 jit_solution(6313304975598689227)
XLA Ops:
  0.0 64.8 %shard_map.46 = bf16[1024,512]{1,0:T(8,128)(2,1)S(1)} custom-call(bf16[1024,512]{1,0:T(8,128)(2,1)} %v_ref.1, s32[4,8]{1,0:T(4,128)} %bitcast.3, s32[4,8]{1,0:T(4,128)} %bitcast.4, s32[1,512]{1,0:T(1,128)} %bitcast.5), custom_call_target="tpu_custom_call" | custom-call | tf_op jit(solution)/shard_map/pallas_call | solution.py:864
  64.8 1.0 %copy.6 = bf16[1024,512]{1,0:T(8,128)(2,1)} copy(bf16[1024,512]{1,0:T(8,128)(2,1)S(1)} %shard_map.46) | data formatting | bytes 2097152
